TPU v7x, 512 devices: a whole 4x4x16 slice. The times are simulated.
512 devices in a mesh: src: 32 (over z, y_hi), tgt: 16 (over y_lo, x, core).
Axes of the slice: x: 4, y: 4 (y_hi: 2, y_lo: 2; y = y_hi * 2 + y_lo), z: 16, core: 2. Of those that a mesh axis runs over, the one named last changes fastest.
Arguments:
- sources: bfloat16 [32768, 512], P('src'), may hold values from -400 to 400
- log_src: float32 [32768], P('src'), may hold values from -1 to 1
- targets: bfloat16 [32768, 512], P(('src', 'tgt')), may hold values from -6 to 6
- potential: float32 [32768], P(('src', 'tgt')), may hold values from -5 to 5
- log_tgt: float32 [32768], P(('src', 'tgt')), may hold values from -1 to 1
Outputs:
- src_pot: float32 [32768], P('src')
- tgt_pot: float32 [32768], P(('src', 'tgt'))
- mapped: bfloat16 [32768, 512], P('src', 'tgt')
All inputs are finite; a program needn't handle non-finite values.
Results may differ from a plain program's by a relative error of at most 0.0144.
Values may be sent and summed in bfloat16 or wider, within the bound.
No kernel may reach another device: no remote copies, remote signals or barrier semaphores. Data moves between devices by JAX's collectives and lax.ppermute only.
A program may use at most 64 MiB of HBM per device.

v0:
```python
import math

import jax
import jax.numpy as jnp
from jax import lax
from jax.experimental import pallas as pl
from jax.experimental.pallas import tpu as pltpu
from jax.sharding import Mesh
from jax.sharding import PartitionSpec as P


WHOLE = pl.BlockSpec(memory_space=pltpu.VMEM)
FAR = pl.BlockSpec(memory_space=pltpu.HBM)
AXES = ("z", "yh", "yl", "x", "c")
PLANE = ("c", "x", "yh", "yl")
CHIPS = ("x", "yh", "yl")
LOG2E = math.log2(math.e)
LN2 = math.log(2.0)
B = 64
A8 = 8
OFF1 = (0, 4, 11, 2, 6, 9, 14, 1, 3, 7, 5, 12)
OFF2 = (15, 8, 13, 10)
OFF = OFF1 + OFF2
PICKS = tuple((m, k) for m, count in enumerate((1, 1, 1, 2, 2, 5, 4)) for k in range(count))
PICKS1 = PICKS[: len(OFF1)]
PICKS2 = PICKS[len(OFF1) :]


MIB = 1 << 20


def params(mib):
    return pltpu.CompilerParams(vmem_limit_bytes=mib * MIB)


def sent(array, axes, pairs):
    return lax.ppermute(array, axes, pairs)


def from_z(array, d):
    n = lax.axis_size("z")
    return sent(array, ("z", "c"), [((i + (d if c == 0 else -d)) % n * 2 + c, i * 2 + c) for i in range(n) for c in (0, 1)])


def split(v):
    hi = v.astype(jnp.bfloat16).astype(jnp.float32)
    lo = (v - hi).astype(jnp.bfloat16).astype(jnp.float32)
    return [hi, lo, v - hi - lo]


def far(array):
    return pltpu.with_memory_space_constraint(array, pltpu.HBM)


def own_kernel(targets, potential, log_tgt, out, pot, log, sems):
    f32, bf = jnp.float32, jnp.bfloat16
    copies = [
        pltpu.make_async_copy(targets, out.at[0:B], sems.at[0]),
        pltpu.make_async_copy(potential, pot, sems.at[1]),
        pltpu.make_async_copy(log_tgt, log, sems.at[2]),
    ]
    for copy in copies:
        copy.start()
    for copy in copies:
        copy.wait()
    rows = []
    for ref in (pot, log):
        rows += split(ref[...])
    extra = jnp.concatenate(rows + [jnp.zeros((2, B), f32)], axis=0).astype(bf)
    out[B : B + A8, :] = jnp.concatenate([extra, jnp.zeros((A8, out.shape[1] - B), bf)], axis=1)


def own_call(targets, potential, log_tgt):
    return pl.pallas_call(
        own_kernel,
        name="own",
        in_specs=[FAR] * 3,
        out_specs=WHOLE,
        out_shape=jax.ShapeDtypeStruct((B + A8, targets.shape[1]), targets.dtype),
        scratch_shapes=[pltpu.VMEM((1, B), jnp.float32)] * 2 + [pltpu.SemaphoreType.DMA((3,))],
        compiler_params=params(4),
    )(*[far(a) for a in (targets, potential.reshape(1, B), log_tgt.reshape(1, B))])


def near_kernel(sources, log_src, out, log, sems):
    n = out.shape[0] - A8
    core = lax.axis_index("c")
    copies = [
        pltpu.make_async_copy(sources.at[pl.ds(pl.multiple_of(core * n, n), n)], out.at[0:n], sems.at[0]),
        pltpu.make_async_copy(log_src, log, sems.at[1]),
    ]
    for copy in copies:
        copy.start()
    for copy in copies:
        copy.wait()
    rows = split(jnp.where(core == 0, log[:, :n], log[:, n:]))
    out[n:, :] = jnp.concatenate(rows + [jnp.zeros((A8 - 3, n), jnp.float32)], axis=0).astype(out.dtype)


def near_call(sources, log_src):
    n, f = sources.shape
    return pl.pallas_call(
        near_kernel,
        name="near_message",
        in_specs=[FAR] * 2,
        out_specs=WHOLE,
        out_shape=jax.ShapeDtypeStruct((n // 2 + A8, f), sources.dtype),
        scratch_shapes=[pltpu.VMEM((1, n), jnp.float32), pltpu.SemaphoreType.DMA((2,))],
        compiler_params=params(4),
    )(far(sources), far(log_src.reshape(1, n)))


def joined(picks, msgs):
    def kernel(*refs):
        out = refs[-1]
        extra = []
        for p, (m, k) in enumerate(picks):
            out[p * B : (p + 1) * B, :] = refs[m][k * B : (k + 1) * B, :]
            extra.append(refs[m][refs[m].shape[0] - A8 :, k * B : (k + 1) * B])
        rest = out.shape[1] - len(picks) * B
        extra.append(jnp.zeros((A8, rest), out.dtype))
        out[len(picks) * B :, :] = jnp.concatenate(extra, axis=1)

    return pl.pallas_call(
        kernel,
        in_specs=[WHOLE] * len(msgs),
        out_specs=WHOLE,
        out_shape=jax.ShapeDtypeStruct((len(picks) * B + A8, msgs[0].shape[1]), msgs[0].dtype),
        compiler_params=params(4),
    )(*msgs)


def eye(n):
    return lax.broadcasted_iota(jnp.int32, (n, n), 0) == lax.broadcasted_iota(jnp.int32, (n, n), 1)


def to_col(row):
    n = row.shape[1]
    return jnp.sum(jnp.where(eye(n), jnp.broadcast_to(row, (n, n)), 0.0), axis=1, keepdims=True)


def to_row(col):
    n = col.shape[0]
    return jnp.sum(jnp.where(eye(n), jnp.broadcast_to(col, (n, n)), 0.0), axis=0, keepdims=True)


CH = 512


def block_of(msgs, m, k):
    extra = msgs[m][msgs[m].shape[0] - A8 :, k * B : (k + 1) * B]
    return msgs[m].at[k * B : (k + 1) * B], extra.astype(jnp.float32)


def row_lse(s_out, at, pot):
    t = pot.shape[0]

    def shifted(r):
        return s_out[r : r + 32, at] + jnp.concatenate([pot[r : r + 32, :]] * (CH // 128), axis=1)

    top = jnp.full((8, CH), -jnp.inf, jnp.float32)
    for r in range(0, t, 32):
        top = jnp.maximum(top, jnp.max(shifted(r).reshape(4, 8, CH), axis=0))
    top = jnp.max(top, axis=0, keepdims=True)
    tot = jnp.zeros((8, CH), jnp.float32)
    for r in range(0, t, 32):
        tot = tot + jnp.sum(jnp.exp2(shifted(r) - top).reshape(4, 8, CH), axis=0)
    return top + jnp.log2(jnp.sum(tot, axis=0, keepdims=True))


def scores(tg, src, scale2):
    return lax.dot_general(tg, src, (((1,), (1,)), ((), ())), preferred_element_type=jnp.float32) * scale2


def laid_out(msgs, picks, tg, pot):
    for p, (m, k) in enumerate(picks):
        rows, ex = block_of(msgs, m, k)
        tg[p * B : (p + 1) * B, :] = rows[...]
        po = (ex[0:1] + ex[1:2] + ex[2:3]) * LOG2E
        pot[p * B : (p + 1) * B, :] = jnp.broadcast_to(to_col(po), (B, 128))


def turned(tg, out, base):
    core = lax.axis_index("c")
    for q in range(tg.shape[0] // 128):
        flipped = tg[q * 128 : (q + 1) * 128, :].T
        for f in range(16):
            to = pl.multiple_of((((f % 2) ^ core) * 8 + f // 2) * 32, 32)
            out[pl.ds(to, 32), base + q * 128 : base + (q + 1) * 128] = flipped[f * 32 : (f + 1) * 32, :]


def own_kernel_first(scale2, sources, *refs):
    msgs, (s_out, lse_out, tgt_out, tg, pot) = refs[:-5], refs[-5:]
    laid_out(msgs, PICKS1, tg, pot)
    for n in range(sources.shape[0] // CH):
        at = slice(n * CH, (n + 1) * CH)
        s_out[:, at] = scores(tg[...], sources[at, :], scale2)
        lse_out[:, at] = row_lse(s_out, at, pot)
    turned(tg, tgt_out, 0)


def near_kernel_first(scale2, near, swapped, log_src, tg, pot, s_out, lse_out, log_out):
    core = lax.axis_index("c")
    halves = []
    for ref in (near, swapped):
        parts = ref[CH:, :].astype(jnp.float32)
        halves.append(parts[0:1] + parts[1:2] + parts[2:3])
    for q in range(8):
        at = slice(q % 4 * 128, (q % 4 + 1) * 128)
        log_out[0, q : q + 1, :] = log_src[:, q * 128 : (q + 1) * 128] * LOG2E
        log_out[1, q : q + 1, :] = jnp.where(core == q // 4, halves[0][:, at], halves[1][:, at]) * LOG2E
    for ref, half in ((near, core), (swapped, 1 - core)):
        at = pl.ds(pl.multiple_of(half * CH, CH), CH)
        s_out[:, at] = scores(tg[...], ref[0:CH, :], scale2)
        lse_out[:, at] = row_lse(s_out, at, pot)


def last_kernel(scale2, sources, near, swapped, lse_own, lse_near, tgt_in, *refs):
    msgs, (s_out, rows_out, tgt_out, lt_out, tg, pot) = refs[:-6], refs[-6:]
    laid_out(msgs, PICKS2, tg, pot)
    yh, core = lax.axis_index("yh"), lax.axis_index("c")
    ns = sources.shape[0]
    for ref, row, lse_in, half, base, block in (
        (sources, 0, lse_own, 0, 0, yh),
        (sources, CH, lse_own, 1, 0, yh),
        (near, 0, lse_near, core, ns, 1 - yh),
        (swapped, 0, lse_near, 1 - core, ns, 1 - yh),
    ):
        begin = half * CH if isinstance(half, int) else pl.multiple_of(half * CH, CH)
        at = pl.ds(base + begin, CH)
        s_out[:, at] = scores(tg[...], ref[row : row + CH, :], scale2)
        lse = added_lse(lse_in[:, pl.ds(begin, CH)], row_lse(s_out, at, pot))
        for i in range(CH // 128):
            piece = jnp.broadcast_to(lse[:, i * 128 : (i + 1) * 128][None], (rows_out.shape[0], 1, 128))
            rows_out[:, block, pl.ds(half * (CH // 128) + i, 1), :] = piece
    for p, (m, k) in enumerate(PICKS):
        _, ex = block_of(msgs, m, k)
        lt_out[p : p + 1, 0:B] = (ex[3:4] + ex[4:5] + ex[5:6]) * LOG2E
    t1 = tgt_in.shape[1]
    tgt_out[:, :t1] = tgt_in[...]
    turned(tg, tgt_out, t1)


def added_lse(a, b):
    top = jnp.maximum(a, b)
    return top + jnp.log2(jnp.exp2(a - top) + jnp.exp2(b - top))


def scores_call(kernel, scale2, args, shapes, scratch, flops):
    return pl.pallas_call(
        lambda *a: kernel(scale2, *a),
        in_specs=[WHOLE] * len(args),
        out_specs=[WHOLE] * len(shapes),
        scratch_shapes=[pltpu.VMEM(s, d) for s, d in scratch],
        out_shape=[jax.ShapeDtypeStruct(s, d) for s, d in shapes],
        compiler_params=params(20),
        cost_estimate=pl.CostEstimate(flops=flops, bytes_accessed=1 << 22, transcendentals=1 << 20),
    )(*args)


def all_scores(sources, log_src, near, swapped, msgs, scale2):
    ns, f = sources.shape
    f32, bf = jnp.float32, jnp.bfloat16
    t1, t2 = len(PICKS1) * B, len(PICKS2) * B
    s1, lse1, tgt1, tg, pot = scores_call(
        own_kernel_first, scale2, [sources, *msgs[:6]],
        [((t1, ns), f32), ((1, ns), f32), ((f, t1), bf), ((t1, f), bf), ((t1, 128), f32)], [], 2 * t1 * ns * f,
    )
    s2, lse2, logs = scores_call(
        near_kernel_first, scale2, [near, swapped, log_src.reshape(1, ns), tg, pot],
        [((t1, ns), f32), ((1, ns), f32), ((2, ns // 128, 128), f32)], [], 2 * t1 * ns * f,
    )
    s3, rows, tgt, lt = scores_call(
        last_kernel, scale2, [sources, near, swapped, lse1, lse2, tgt1, *msgs],
        [((t2, 2 * ns), f32), ((32, 2, ns // 128, 128), f32), ((f, t1 + t2), bf), ((len(OFF), 128), f32)],
        [((t2, f), bf), ((t2, 128), f32)], 4 * t2 * ns * f,
    )
    return (s1, s2, s3), rows, logs, tgt, lt


def merged_lse(parts):
    top = jnp.max(parts, axis=0)
    return top + jnp.log2(jnp.sum(jnp.exp2(parts - top[None]), axis=0))


def slot_of(p):
    off = jnp.where(lax.axis_index("c") == 0, OFF[p], 16 - OFF[p])
    return (lax.axis_index("z") + off) % 16


def cols_kernel(parts, logs, s1, s2, s3, sp_out, msg_out, held, lse):
    yh = lax.axis_index("yh")
    for h in range(2):
        lse[h] = merged_lse(parts[:, h])
    for h, block in enumerate((yh, 1 - yh)):
        sp = logs[h] - lse[block]
        for r in range(8):
            sp_out[:, (h * 8 + r) * 128 : (h * 8 + r + 1) * 128] = sp[r : r + 1, :]
    held[...] = jnp.zeros_like(held)
    n1 = len(OFF1)
    ns = s1.shape[1]
    for p in range(len(OFF)):
        tops, totals = [], []
        for r in range(0, B, 8):
            lifted = []
            for k in range(2 * ns // 128):
                ref, base, col = (s3, (p - n1) * B, k * 128)
                if p < n1:
                    ref, base, col = (s1, p * B, k * 128) if k * 128 < ns else (s2, p * B, k * 128 - ns)
                lifted.append(ref[base + r : base + r + 8, col : col + 128] + sp_out[:, k * 128 : (k + 1) * 128])
            top = lifted[0]
            for v in lifted[1:]:
                top = jnp.maximum(top, v)
            total = jnp.exp2(lifted[0] - top)
            for v in lifted[1:]:
                total = total + jnp.exp2(v - top)
            tops.append(top)
            totals.append(total)
        tops, totals = jnp.concatenate(tops, axis=0), jnp.concatenate(totals, axis=0)
        top = jnp.max(tops, axis=1, keepdims=True)
        row = to_row(top + jnp.log2(jnp.sum(totals * jnp.exp2(tops - top), axis=1, keepdims=True)))
        row = jnp.concatenate([row, row], axis=1)
        slot = slot_of(p)
        at = slot // 2
        half = lax.broadcasted_iota(jnp.int32, (1, 128), 1) // B
        held[pl.ds(at, 1), :] = jnp.where(half == slot % 2, row, held[pl.ds(at, 1), :])
    msg_out[...] = jnp.broadcast_to(held[...][None], msg_out.shape)


def cols_call(parts, logs, s):
    ns = s[2].shape[1]
    return pl.pallas_call(
        cols_kernel,
        name="cols",
        in_specs=[WHOLE] * 5,
        out_specs=[WHOLE] * 2,
        scratch_shapes=[pltpu.VMEM((8, 128), jnp.float32), pltpu.VMEM((2, 8, 128), jnp.float32)],
        out_shape=[jax.ShapeDtypeStruct((1, ns), jnp.float32), jax.ShapeDtypeStruct((16, 8, 128), jnp.float32)],
        compiler_params=params(16),
    )(parts, logs, *s)


def moved_kernel(parts, lt, sp, s1, s2, s3, tgt, pot_out, theirs_out, mass_out, wide, tp, lse):
    lse[...] = merged_lse(parts[...])
    for p in range(len(OFF)):
        slot = slot_of(p)
        row = lse[pl.ds(slot // 2, 1), :]
        row = jnp.where(slot % 2 == 0, row[:, :B], row[:, B:])
        tpot = lt[p : p + 1, 0:B] - row
        if p == 0:
            pot_out[:, 0:B] = tpot * LN2
        tp[p * B : (p + 1) * B, :] = jnp.broadcast_to(to_col(tpot), (B, 128))

    t1, ns = s1.shape
    half = tgt.shape[0] // 2
    for n in range(sp.shape[1] // CH):
        at = slice(n * CH, (n + 1) * CH)
        spn = sp[:, at]
        mass = jnp.zeros((8, CH), jnp.float32)
        for r in range(0, tp.shape[0], 32):
            if r >= t1:
                s = s3[r - t1 : r - t1 + 32, at]
            elif n * CH < ns:
                s = s1[r : r + 32, at]
            else:
                s = s2[r : r + 32, n * CH - ns : (n + 1) * CH - ns]
            e = jnp.exp2(s + spn + jnp.concatenate([tp[r : r + 32, :]] * (CH // 128), axis=1))
            mass = mass + jnp.sum(e.reshape(4, 8, CH), axis=0)
            wide[r : r + 32, at] = e.astype(jnp.bfloat16)
        mass = jnp.sum(mass, axis=0, keepdims=True)
        mass_out[:, at] = mass
        part = jnp.dot(tgt[half:, :], wide[:, at], preferred_element_type=jnp.float32)
        theirs_out[0:half, at] = part.astype(jnp.bfloat16)
        hi = mass.astype(jnp.bfloat16).astype(jnp.float32)
        pad = jnp.zeros((6, CH), jnp.float32)
        theirs_out[half : half + 8, at] = jnp.concatenate([hi, mass - hi, pad], axis=0).astype(jnp.bfloat16)


def moved_call(parts, lt, sp, s, tgt):
    ns = sp.shape[1]
    f, t = tgt.shape
    return pl.pallas_call(
        moved_kernel,
        name="moved",
        in_specs=[WHOLE] * 7,
        out_specs=[WHOLE] * 4,
        scratch_shapes=[pltpu.VMEM((t, 128), jnp.float32), pltpu.VMEM((8, 128), jnp.float32)],
        out_shape=[
            jax.ShapeDtypeStruct((1, 128), jnp.float32),
            jax.ShapeDtypeStruct((f // 2 + 8, ns), jnp.bfloat16),
            jax.ShapeDtypeStruct((1, ns), jnp.float32),
            jax.ShapeDtypeStruct((t, ns), jnp.bfloat16),
        ],
        compiler_params=params(20),
    )(parts, lt, sp, *s, tgt)


def mine_kernel(tgt, wide, out):
    for n in range(out.shape[1] // CH):
        at = slice(n * CH, (n + 1) * CH)
        part = jnp.dot(tgt[: out.shape[0], :], wide[:, at], preferred_element_type=jnp.float32)
        out[:, at] = part.astype(jnp.bfloat16)


def mine_call(tgt, wide):
    f, t = tgt.shape
    ns = wide.shape[1]
    return pl.pallas_call(
        mine_kernel,
        name="mine",
        in_specs=[WHOLE] * 2,
        out_specs=WHOLE,
        out_shape=jax.ShapeDtypeStruct((f // 2, ns), jnp.bfloat16),
        compiler_params=params(12),
        cost_estimate=pl.CostEstimate(flops=f * t * ns, bytes_accessed=2 * t * ns, transcendentals=0),
    )(tgt, wide)


def pack_kernel(mine, theirs, mass, out):
    f32 = jnp.float32
    extra = theirs[256:264, :].astype(f32)
    total = mass[...] + extra[0:1] + extra[1:2]
    hi = total.astype(jnp.bfloat16).astype(f32)
    lo = total - hi
    yh = lax.axis_index("yh")
    for h in range(2):
        to = (h ^ yh) * 2
        rows = [v[:, (h * 8 + q) * 128 : (h * 8 + q + 1) * 128] for v in (hi, lo) for q in range(8)]
        rows = jnp.concatenate(rows, axis=0).astype(jnp.bfloat16)
        for g in range(8):
            at_chip = g % 4 * 4 + g // 4
            for q in range(8):
                at = (slice(g * 32, (g + 1) * 32), slice((h * 8 + q) * 128, (h * 8 + q + 1) * 128))
                both = mine[at].astype(f32) + theirs[at].astype(f32)
                out[to + at_chip, q * 32 : (q + 1) * 32, :] = both.astype(jnp.bfloat16)
            out[to + at_chip, 256:272, :] = rows


def pack_call(mine, theirs, mass):
    return pl.pallas_call(
        pack_kernel,
        name="pack",
        in_specs=[WHOLE] * 3,
        out_specs=WHOLE,
        out_shape=jax.ShapeDtypeStruct((16, 272, 128), jnp.bfloat16),
        compiler_params=params(8),
    )(mine, theirs, mass)


def finish_kernel(parts, sp, tpot, out, src_pot, tgt_pot):
    f32 = jnp.float32

    def added(at):
        total = parts[0, at, :].astype(f32)
        for k in range(1, parts.shape[0]):
            total = total + parts[k, at, :].astype(f32)
        return total

    for q in range(8):
        src_pot[q : q + 1, :] = sp[:, q * 128 : (q + 1) * 128] * LN2
    tgt_pot[...] = tpot[:, 0:B]
    mass = added(slice(256, 272))
    mass = mass[:8] + mass[8:]
    for q in range(8):
        image = added(slice(q * 32, (q + 1) * 32)) / mass[q : q + 1, :]
        out[:, q * 128 : (q + 1) * 128] = image.astype(jnp.bfloat16)


def finish_call(parts, sp, tpot):
    return pl.pallas_call(
        finish_kernel,
        name="finish",
        in_specs=[WHOLE] * 3,
        out_specs=[WHOLE] * 3,
        out_shape=[
            jax.ShapeDtypeStruct((32, 1024), jnp.bfloat16),
            jax.ShapeDtypeStruct((8, 128), jnp.float32),
            jax.ShapeDtypeStruct((1, B), jnp.float32),
        ],
        compiler_params=params(8),
    )(parts, sp, tpot)


def body(sources, log_src, targets, potential, log_tgt):
    f = sources.shape[1]
    scale2 = LOG2E / math.sqrt(f)

    own = own_call(targets, potential, log_tgt)
    ra = from_z(own, 4)
    la = from_z(own, -5)
    near = sent(near_call(sources, log_src), ("yh", "yl"), [(0, 3), (3, 0), (1, 2), (2, 1)])
    rb = from_z(joined([(0, 0), (1, 0)], [own, ra]), 2)
    lb = from_z(joined([(1, 0), (0, 0)], [own, la]), -2)
    rc = from_z(joined([(0, 0), (1, 0), (1, 1), (2, 0), (3, 0)], [own, rb, ra, la]), 1)
    lc = from_z(joined([(0, 0), (1, 0), (1, 1), (2, 0)], [own, lb, la]), -1)
    swapped = sent(near, "c", [(0, 1), (1, 0)])
    s, rows, logs, tgt, lt = all_scores(sources, log_src, near, swapped, [own, ra, la, rb, lb, rc, lc], scale2)
    row_parts = lax.all_to_all(rows, PLANE, split_axis=0, concat_axis=0, tiled=True)
    sp, cols = cols_call(row_parts, logs, s)
    col_parts = lax.all_to_all(cols, "z", split_axis=0, concat_axis=0, tiled=True)
    tpot, theirs, mass, wide = moved_call(col_parts, lt, sp, s, tgt)
    theirs = lax.ppermute(theirs, "c", [(0, 1), (1, 0)])
    packed = pack_call(mine_call(tgt, wide), theirs, mass)
    parts = lax.all_to_all(packed, CHIPS, split_axis=0, concat_axis=0, tiled=True)
    mapped, src_pot, tgt_pot = finish_call(parts, sp, tpot)
    return (src_pot.reshape(-1), tgt_pot.reshape(-1), mapped.T)


def solution(mesh):
    torus = Mesh(mesh.devices.reshape(16, 2, 2, 4, 2), AXES)
    src, every = ("z", "yh"), ("z", "yh", "yl", "x", "c")
    return jax.shard_map(
        body,
        mesh=torus,
        in_specs=(P(src, None), P(src), P(every, None), P(every), P(every)),
        out_specs=(P(src), P(every), P(src, ("yl", "x", "c"))),
        check_vma=False,
    )
```

profile of v0, /device:TPU:1, one launch (start us, length us, event | category | flops | bytes accessed | tf_op | source)
XLA Modules:
  0.0 134.2 jit_solution(13270409553721771057)
XLA Ops:
  0.6 1.2 near_message.1
  1.8 5.5 %collective-permute-start = (bf16[520,512]{1,0:T(8,128)(2,1)S(1)}, bf16[520,512]{1,0:T(8,128)(2,1)S(1)}, u32[]{:S(2)}, u32[]{:S(2)}) collective-permute-start(bf16[520,512]{1,0:T(8,128)(2,1)S(1)} %near_message.1), channel_id=1, source_target_pairs={{0,24},{24,0},{8,16},{16,8},{1,25},{25,1},{9,17},{17,9},{2,26},{26... | collective-permute-start | bytes 1597448 | tf_op jit(solution)/shard_map/ppermute | solution.py:37
  7.3 0.9 own.1.refs_0_.a_1_.a_6_
  8.2 8.8 %collective-permute-start.2 = (bf16[72,512]{1,0:T(8,128)(2,1)S(1)}, bf16[72,512]{1,0:T(8,128)(2,1)S(1)}, u32[]{:S(2)}, u32[]{:S(2)}) collective-permute-start(bf16[72,512]{1,0:T(8,128)(2,1)S(1)} %own.1.refs_0_.a_1_.a_6_), channel_id=1, source_target_pairs={{128,0},{385,1},{160,32},{417,33},{192,64},{449,65},{224,96},{481,... | collective-permute-start | bytes 221192 | tf_op jit(solution)/shard_map/ppermute | solution.py:37
  17.0 5.7 %collective-permute-done.2.refs_1_.refs_2_.a_2_.a_7_ = bf16[72,512]{1,0:T(8,128)(2,1)S(1)} collective-permute-done((bf16[72,512]{1,0:T(8,128)(2,1)S(1)}, bf16[72,512]{1,0:T(8,128)(2,1)S(1)}, u32[]{:S(2)}, u32[]{:S(2)}) %collective-permute-start.2) | collective-permute-done | bytes 73760 | tf_op jit(solution)/shard_map/ppermute | solution.py:37
  22.8 4.6 %collective-permute-start.4 = (bf16[136,512]{1,0:T(8,128)(2,1)S(1)}, bf16[136,512]{1,0:T(8,128)(2,1)S(1)}, u32[]{:S(2)}, u32[]{:S(2)}) collective-permute-start(bf16[136,512]{1,0:T(8,128)(2,1)S(1)} %shard_map.76), channel_id=1, source_target_pairs={{64,0},{449,1},{96,32},{481,33},{128,64},{1,65},{160,96},{33,97},{... | collective-permute-start | bytes 417800 | tf_op jit(solution)/shard_map/ppermute | solution.py:37
  27.4 6.9 %collective-permute-start.1 = (bf16[520,512]{1,0:T(8,128)(2,1)S(1)}, bf16[520,512]{1,0:T(8,128)(2,1)S(1)}, u32[]{:S(2)}, u32[]{:S(2)}) collective-permute-start(bf16[520,512]{1,0:T(8,128)(2,1)S(1)} %collective-permute-done.a_0_.a_1_), channel_id=1, source_target_pairs={{0,1},{1,0},{2,3},{3,2},{4,5},{5,4},{6,7},{7,6},{8,9},{9,8},{10,11... | collective-permute-start | bytes 1597448 | tf_op jit(solution)/shard_map/ppermute | solution.py:37
  34.3 6.3 %collective-permute-start.3 = (bf16[72,512]{1,0:T(8,128)(2,1)S(1)}, bf16[72,512]{1,0:T(8,128)(2,1)S(1)}, u32[]{:S(2)}, u32[]{:S(2)}) collective-permute-start(bf16[72,512]{1,0:T(8,128)(2,1)S(1)} %own.1.refs_0_.a_1_.a_6_), channel_id=1, source_target_pairs={{352,0},{161,1},{384,32},{193,33},{416,64},{225,65},{448,96},{257,... | collective-permute-start | bytes 221192 | tf_op jit(solution)/shard_map/ppermute | solution.py:37
  40.6 4.4 %collective-permute-done.3.refs_1_.refs_3_.a_3_.refs_2_.a_8_ = bf16[72,512]{1,0:T(8,128)(2,1)S(1)} collective-permute-done((bf16[72,512]{1,0:T(8,128)(2,1)S(1)}, bf16[72,512]{1,0:T(8,128)(2,1)S(1)}, u32[]{:S(2)}, u32[]{:S(2)}) %collective-permute-start.3) | collective-permute-done | bytes 73760 | tf_op jit(solution)/shard_map/ppermute | solution.py:37
  45.1 3.0 %collective-permute-start.6 = (bf16[328,512]{1,0:T(8,128)(2,1)S(1)}, bf16[328,512]{1,0:T(8,128)(2,1)S(1)}, u32[]{:S(2)}, u32[]{:S(2)}) collective-permute-start(bf16[328,512]{1,0:T(8,128)(2,1)S(1)} %shard_map.78), channel_id=1, source_target_pairs={{32,0},{481,1},{64,32},{1,33},{96,64},{33,65},{128,96},{65,97},{16... | collective-permute-start | bytes 1007624 | tf_op jit(solution)/shard_map/ppermute | solution.py:37
  48.2 5.5 %collective-permute-start.5 = (bf16[136,512]{1,0:T(8,128)(2,1)S(1)}, bf16[136,512]{1,0:T(8,128)(2,1)S(1)}, u32[]{:S(2)}, u32[]{:S(2)}) collective-permute-start(bf16[136,512]{1,0:T(8,128)(2,1)S(1)} %shard_map.77), channel_id=1, source_target_pairs={{448,0},{65,1},{480,32},{97,33},{0,64},{129,65},{32,96},{161,97},{... | collective-permute-start | bytes 417800 | tf_op jit(solution)/shard_map/ppermute | solution.py:37
  53.7 3.9 %collective-permute-done.5.a_5_.refs_1_.a_10_ = bf16[136,512]{1,0:T(8,128)(2,1)S(1)} collective-permute-done((bf16[136,512]{1,0:T(8,128)(2,1)S(1)}, bf16[136,512]{1,0:T(8,128)(2,1)S(1)}, u32[]{:S(2)}, u32[]{:S(2)}) %collective-permute-start.5) | collective-permute-done | bytes 139296 | tf_op jit(solution)/shard_map/ppermute | solution.py:37
  57.7 5.7 %collective-permute-start.7 = (bf16[264,512]{1,0:T(8,128)(2,1)S(1)}, bf16[264,512]{1,0:T(8,128)(2,1)S(1)}, u32[]{:S(2)}, u32[]{:S(2)}) collective-permute-start(bf16[264,512]{1,0:T(8,128)(2,1)S(1)} %shard_map.81), channel_id=1, source_target_pairs={{480,0},{33,1},{0,32},{65,33},{32,64},{97,65},{64,96},{129,97},{96... | collective-permute-start | bytes 811016 | tf_op jit(solution)/shard_map/ppermute | solution.py:37
  63.4 1.6 %shard_map.79 = (f32[768,1024]{1,0:T(8,128)S(1)}, f32[1,1024]{1,0:T(1,128)S(1)}, bf16[512,768]{1,0:T(8,128)(2,1)S(1)}, bf16[768,512]{1,0:T(8,128)(2,1)S(1)}, f32[768,128]{1,0:T(8,128)S(1)}) custom-call(bf16[1024,512]{1,0:T(8,128)(2,1)S(1)} %copy-done, bf16[72,512]{1,0:T(8,128)(2,1)S(1)} %own.1.refs_0_.a_1_.a_6_, ...), custom_call_target="tpu_custom_call" | custom-call | flops 805306368 | bytes 4194304 | tf_op jit(solution)/shard_map/pallas_call | solution.py:250
  65.0 1.5 %shard_map.80 = (f32[768,1024]{1,0:T(8,128)S(1)}, f32[1,1024]{1,0:T(1,128)S(1)}, f32[2,8,128]{2,1,0:T(8,128)S(1)}) custom-call(bf16[520,512]{1,0:T(8,128)(2,1)S(1)} %collective-permute-done.a_0_.a_1_, bf16[520,512]{1,0:T(8,128)(2,1)S(1)} %collective-permute-done.1.a_1_.a_2_, f32[1,1024]{1,0:T(1,128)S(1)} %bitcast.7, ...), custom_call_target="tpu_custom_call" | custom-call | flops 805306368 | bytes 4194304 | tf_op jit(solution)/shard_map/pallas_call | solution.py:250
  66.7 1.3 shard_map.82
  68.1 17.0 %all_to_all.15.parts = f32[32,2,8,128]{3,2,1,0:T(8,128)S(1)} all-to-all(f32[32,2,8,128]{3,2,1,0:T(8,128)S(1)} %get-tuple-element.30), channel_id=1, replica_groups=mesh['z'=16,'yh'=2,'yl'=2,'x'=4,'c'=2] {'c','x','yh','yl'}, dimensions={0} | all-to-all | bytes 524288 | tf_op jit(solution)/shard_map/all_to_all | solution.py:498
  85.0 2.1 %cols.1 = (f32[1,2048]{1,0:T(1,128)S(1)}, f32[16,8,128]{2,1,0:T(8,128)S(1)}) custom-call(f32[32,2,8,128]{3,2,1,0:T(8,128)S(1)} %all_to_all.15.parts, f32[2,8,128]{2,1,0:T(8,128)S(1)} %get-tuple-element.31.logs, f32[768,1024]{1,0:T(8,128)S(1)} %get-tuple-element.32.s1, f32[768,1024]{1,0:T(8,128)S(1)} %get-tuple-element.33.s2, ...), custom_call_target="tpu_custom_call" | custom-call | tf_op jit(solution)/shard_map/cols/pallas_call | solution.py:332
  87.2 17.2 %all_to_all.16.parts = f32[16,8,128]{2,1,0:T(8,128)S(1)} all-to-all(f32[16,8,128]{2,1,0:T(8,128)S(1)} %get-tuple-element.35), channel_id=1, replica_groups=mesh['z'=16,'yh'=2,'yl'=2,'x'=4,'c'=2] {'z'}, dimensions={0} | all-to-all | bytes 131072 | tf_op jit(solution)/shard_map/all_to_all | solution.py:500
  104.4 2.3 %moved.1 = (f32[1,128]{1,0:T(1,128)S(1)}, bf16[264,2048]{1,0:T(8,128)(2,1)S(1)}, f32[1,2048]{1,0:T(1,128)S(1)}, bf16[1024,2048]{1,0:T(8,128)(2,1)S(1)}) custom-call(f32[16,8,128]{2,1,0:T(8,128)S(1)} %all_to_all.16.parts, f32[16,128]{1,0:T(8,128)S(1)} %get-tuple-element.36.lt, f32[1,2048]{1,0:T(1,128)S(1)} %get-tuple-element.37.sp, ...), custom_call_target="tpu_custom_call" | custom-call | tf_op jit(solution)/shard_map/moved/pallas_call | solution.py:382
  106.7 3.9 %collective-permute-start.8 = (bf16[264,2048]{1,0:T(8,128)(2,1)S(1)}, bf16[264,2048]{1,0:T(8,128)(2,1)S(1)}, u32[]{:S(2)}, u32[]{:S(2)}) collective-permute-start(bf16[264,2048]{1,0:T(8,128)(2,1)S(1)} %get-tuple-element.39), channel_id=1, source_target_pairs={{0,1},{1,0},{2,3},{3,2},{4,5},{5,4},{6,7},{7,6},{8,9},{9,8},{10,11... | collective-permute-start | bytes 3244040 | tf_op jit(solution)/shard_map/ppermute | solution.py:502
  110.6 1.3 mine.1
  111.9 1.0 collective-permute-done.8.theirs
  113.2 20.2 %all_to_all.17.parts = bf16[16,272,128]{2,1,0:T(8,128)(2,1)S(1)} all-to-all(bf16[16,272,128]{2,1,0:T(8,128)(2,1)S(1)} %pack.1), channel_id=1, replica_groups=mesh['z'=16,'yh'=2,'yl'=2,'x'=4,'c'=2] {'x','yh','yl'}, dimensions={0} | all-to-all | bytes 2228224 | tf_op jit(solution)/shard_map/all_to_all | solution.py:504
  (15 shorter events, 1.7 us)
Async XLA Ops:
  0.6 62.7 %copy-start = (bf16[1024,512]{1,0:T(8,128)(2,1)S(1)}, bf16[1024,512]{1,0:T(8,128)(2,1)}, u32[]{:S(2)}) copy-start(bf16[1024,512]{1,0:T(8,128)(2,1)} %a_0_.3) | copy-start | bytes 3145732
  1.8 25.5 %collective-permute-start = (bf16[520,512]{1,0:T(8,128)(2,1)S(1)}, bf16[520,512]{1,0:T(8,128)(2,1)S(1)}, u32[]{:S(2)}, u32[]{:S(2)}) collective-permute-start(bf16[520,512]{1,0:T(8,128)(2,1)S(1)} %near_message.1), channel_id=1, source_target_pairs={{0,24},{24,0},{8,16},{16,8},{1,25},{25,1},{9,17},{17,9},{2,26},{26... | collective-permute-start | bytes 1597448 | tf_op jit(solution)/shard_map/ppermute | solution.py:37
  8.2 14.5 %collective-permute-start.2 = (bf16[72,512]{1,0:T(8,128)(2,1)S(1)}, bf16[72,512]{1,0:T(8,128)(2,1)S(1)}, u32[]{:S(2)}, u32[]{:S(2)}) collective-permute-start(bf16[72,512]{1,0:T(8,128)(2,1)S(1)} %own.1.refs_0_.a_1_.a_6_), channel_id=1, source_target_pairs={{128,0},{385,1},{160,32},{417,33},{192,64},{449,65},{224,96},{481,... | collective-permute-start | bytes 221192 | tf_op jit(solution)/shard_map/ppermute | solution.py:37
  22.8 42.2 %copy-start.1 = (f32[1024]{0:T(1024)S(1)}, f32[1024]{0:T(1024)}, u32[]{:S(2)}) copy-start(f32[1024]{0:T(1024)} %param.6) | copy-start | bytes 12292
  22.8 22.2 %collective-permute-start.4 = (bf16[136,512]{1,0:T(8,128)(2,1)S(1)}, bf16[136,512]{1,0:T(8,128)(2,1)S(1)}, u32[]{:S(2)}, u32[]{:S(2)}) collective-permute-start(bf16[136,512]{1,0:T(8,128)(2,1)S(1)} %shard_map.76), channel_id=1, source_target_pairs={{64,0},{449,1},{96,32},{481,33},{128,64},{1,65},{160,96},{33,97},{... | collective-permute-start | bytes 417800 | tf_op jit(solution)/shard_map/ppermute | solution.py:37
  27.4 37.6 %collective-permute-start.1 = (bf16[520,512]{1,0:T(8,128)(2,1)S(1)}, bf16[520,512]{1,0:T(8,128)(2,1)S(1)}, u32[]{:S(2)}, u32[]{:S(2)}) collective-permute-start(bf16[520,512]{1,0:T(8,128)(2,1)S(1)} %collective-permute-done.a_0_.a_1_), channel_id=1, source_target_pairs={{0,1},{1,0},{2,3},{3,2},{4,5},{5,4},{6,7},{7,6},{8,9},{9,8},{10,11... | collective-permute-start | bytes 1597448 | tf_op jit(solution)/shard_map/ppermute | solution.py:37
  34.3 10.7 %collective-permute-start.3 = (bf16[72,512]{1,0:T(8,128)(2,1)S(1)}, bf16[72,512]{1,0:T(8,128)(2,1)S(1)}, u32[]{:S(2)}, u32[]{:S(2)}) collective-permute-start(bf16[72,512]{1,0:T(8,128)(2,1)S(1)} %own.1.refs_0_.a_1_.a_6_), channel_id=1, source_target_pairs={{352,0},{161,1},{384,32},{193,33},{416,64},{225,65},{448,96},{257,... | collective-permute-start | bytes 221192 | tf_op jit(solution)/shard_map/ppermute | solution.py:37
  45.1 18.3 %collective-permute-start.6 = (bf16[328,512]{1,0:T(8,128)(2,1)S(1)}, bf16[328,512]{1,0:T(8,128)(2,1)S(1)}, u32[]{:S(2)}, u32[]{:S(2)}) collective-permute-start(bf16[328,512]{1,0:T(8,128)(2,1)S(1)} %shard_map.78), channel_id=1, source_target_pairs={{32,0},{481,1},{64,32},{1,33},{96,64},{33,65},{128,96},{65,97},{16... | collective-permute-start | bytes 1007624 | tf_op jit(solution)/shard_map/ppermute | solution.py:37
  48.2 9.4 %collective-permute-start.5 = (bf16[136,512]{1,0:T(8,128)(2,1)S(1)}, bf16[136,512]{1,0:T(8,128)(2,1)S(1)}, u32[]{:S(2)}, u32[]{:S(2)}) collective-permute-start(bf16[136,512]{1,0:T(8,128)(2,1)S(1)} %shard_map.77), channel_id=1, source_target_pairs={{448,0},{65,1},{480,32},{97,33},{0,64},{129,65},{32,96},{161,97},{... | collective-permute-start | bytes 417800 | tf_op jit(solution)/shard_map/ppermute | solution.py:37
  57.7 9.1 %collective-permute-start.7 = (bf16[264,512]{1,0:T(8,128)(2,1)S(1)}, bf16[264,512]{1,0:T(8,128)(2,1)S(1)}, u32[]{:S(2)}, u32[]{:S(2)}) collective-permute-start(bf16[264,512]{1,0:T(8,128)(2,1)S(1)} %shard_map.81), channel_id=1, source_target_pairs={{480,0},{33,1},{0,32},{65,33},{32,64},{97,65},{64,96},{129,97},{96... | collective-permute-start | bytes 811016 | tf_op jit(solution)/shard_map/ppermute | solution.py:37
  106.7 6.3 %collective-permute-start.8 = (bf16[264,2048]{1,0:T(8,128)(2,1)S(1)}, bf16[264,2048]{1,0:T(8,128)(2,1)S(1)}, u32[]{:S(2)}, u32[]{:S(2)}) collective-permute-start(bf16[264,2048]{1,0:T(8,128)(2,1)S(1)} %get-tuple-element.39), channel_id=1, source_target_pairs={{0,1},{1,0},{2,3},{3,2},{4,5},{5,4},{6,7},{7,6},{8,9},{9,8},{10,11... | collective-permute-start | bytes 3244040 | tf_op jit(solution)/shard_map/ppermute | solution.py:502
where the time goes:
time: 135 us; the launch traced here: 134 us
  blocking collectives  54.4 us (40%)
  starting transfers between devices  50.2 us (37%)
  waiting for transfers between devices  15.3 us (11%)
  Pallas kernels  13.5 us (10%)
    ppermute x8, starting transfers between devices, sent(): return lax.ppermute(array, axes, pairs)  46.3 us
    all_to_all x1, blocking collectives, body(): lax.all_to_all(packed, CHIPS, split_axis=0, concat_axis=0, tiled=True)  20.2 us
    all_to_all x1, blocking collectives, body(): lax.all_to_all(cols, 'z', split_axis=0, concat_axis=0, tiled=True)  17.2 us
    all_to_all x1, blocking collectives, body(): lax.all_to_all(rows, PLANE, split_axis=0, concat_axis=0, tiled=True)  17 us
    ppermute x8, waiting for transfers between devices, sent(): return lax.ppermute(array, axes, pairs)  14.2 us
    pallas_call x3, Pallas kernels, scores_call(): pl.pallas_call(lambda *a: kernel(scale2, *a), in_specs=[WHOLE] * len(args...  4.39 us
    ppermute x1, starting transfers between devices, body(): theirs = lax.ppermute(theirs, 'c', [(0, 1), (1, 0)])  3.95 us
  transfers between devices with their start and end apart: 9, of which 5 were waited for; matrix products, arithmetic and copies ran while one was open for 0% of the time, Pallas kernels for 4%

commit v1 on v0

--- a/solution.py
+++ b/solution.py
@@ -13,7 +13,7 @@
 FAR = pl.BlockSpec(memory_space=pltpu.HBM)
 AXES = ("z", "yh", "yl", "x", "c")
 PLANE = ("c", "x", "yh", "yl")
-CHIPS = ("x", "yh", "yl")
+CHIPS = ("yl", "yh", "x")
 LOG2E = math.log2(math.e)
 LN2 = math.log(2.0)
 B = 64
@@ -424,11 +424,11 @@
     lo = total - hi
     yh = lax.axis_index("yh")
     for h in range(2):
-        to = (h ^ yh) * 2
+        to = (h ^ yh) * 4
         rows = [v[:, (h * 8 + q) * 128 : (h * 8 + q + 1) * 128] for v in (hi, lo) for q in range(8)]
         rows = jnp.concatenate(rows, axis=0).astype(jnp.bfloat16)
         for g in range(8):
-            at_chip = g % 4 * 4 + g // 4
+            at_chip = g // 4 * 8 + g % 4
             for q in range(8):
                 at = (slice(g * 32, (g + 1) * 32), slice((h * 8 + q) * 128, (h * 8 + q + 1) * 128))
                 both = mine[at].astype(f32) + theirs[at].astype(f32)

time: 135 us -> 135 us (level)
  no operation moved by 1% of the time
where the time goes in v1:
time: 135 us; the launch traced here: 134 us
  blocking collectives  54.3 us (40%)
  starting transfers between devices  50.2 us (37%)
  waiting for transfers between devices  15.3 us (11%)
  Pallas kernels  13.5 us (10%)
    ppermute x8, starting transfers between devices, sent(): return lax.ppermute(array, axes, pairs)  46.3 us
    all_to_all x1, blocking collectives, body(): lax.all_to_all(packed, CHIPS, split_axis=0, concat_axis=0, tiled=True)  20.2 us
    all_to_all x1, blocking collectives, body(): lax.all_to_all(cols, 'z', split_axis=0, concat_axis=0, tiled=True)  17.2 us
    all_to_all x1, blocking collectives, body(): lax.all_to_all(rows, PLANE, split_axis=0, concat_axis=0, tiled=True)  17 us
    ppermute x8, waiting for transfers between devices, sent(): return lax.ppermute(array, axes, pairs)  14.2 us
    pallas_call x3, Pallas kernels, scores_call(): pl.pallas_call(lambda *a: kernel(scale2, *a), in_specs=[WHOLE] * len(args...  4.39 us
    ppermute x1, starting transfers between devices, body(): theirs = lax.ppermute(theirs, 'c', [(0, 1), (1, 0)])  3.95 us
  transfers between devices with their start and end apart: 9, of which 5 were waited for; matrix products, arithmetic and copies ran while one was open for 0% of the time, Pallas kernels for 4%

profile of v1, /device:TPU:1, one launch (start us, length us, event | category | flops | bytes accessed | tf_op | source)
XLA Modules:
  0.0 134.2 jit_solution(8144648187237727344)
XLA Ops:
  0.6 1.2 near_message.1
  1.8 5.5 %collective-permute-start = (bf16[520,512]{1,0:T(8,128)(2,1)S(1)}, bf16[520,512]{1,0:T(8,128)(2,1)S(1)}, u32[]{:S(2)}, u32[]{:S(2)}) collective-permute-start(bf16[520,512]{1,0:T(8,128)(2,1)S(1)} %near_message.1), channel_id=1, source_target_pairs={{0,24},{24,0},{8,16},{16,8},{1,25},{25,1},{9,17},{17,9},{2,26},{26... | collective-permute-start | bytes 1597448 | tf_op jit(solution)/shard_map/ppermute | solution.py:37
  7.3 0.9 own.1.refs_0_.a_1_.a_6_
  8.2 8.8 %collective-permute-start.2 = (bf16[72,512]{1,0:T(8,128)(2,1)S(1)}, bf16[72,512]{1,0:T(8,128)(2,1)S(1)}, u32[]{:S(2)}, u32[]{:S(2)}) collective-permute-start(bf16[72,512]{1,0:T(8,128)(2,1)S(1)} %own.1.refs_0_.a_1_.a_6_), channel_id=1, source_target_pairs={{128,0},{385,1},{160,32},{417,33},{192,64},{449,65},{224,96},{481,... | collective-permute-start | bytes 221192 | tf_op jit(solution)/shard_map/ppermute | solution.py:37
  17.0 5.7 %collective-permute-done.2.refs_1_.refs_2_.a_2_.a_7_ = bf16[72,512]{1,0:T(8,128)(2,1)S(1)} collective-permute-done((bf16[72,512]{1,0:T(8,128)(2,1)S(1)}, bf16[72,512]{1,0:T(8,128)(2,1)S(1)}, u32[]{:S(2)}, u32[]{:S(2)}) %collective-permute-start.2) | collective-permute-done | bytes 73760 | tf_op jit(solution)/shard_map/ppermute | solution.py:37
  22.8 4.6 %collective-permute-start.4 = (bf16[136,512]{1,0:T(8,128)(2,1)S(1)}, bf16[136,512]{1,0:T(8,128)(2,1)S(1)}, u32[]{:S(2)}, u32[]{:S(2)}) collective-permute-start(bf16[136,512]{1,0:T(8,128)(2,1)S(1)} %shard_map.76), channel_id=1, source_target_pairs={{64,0},{449,1},{96,32},{481,33},{128,64},{1,65},{160,96},{33,97},{... | collective-permute-start | bytes 417800 | tf_op jit(solution)/shard_map/ppermute | solution.py:37
  27.4 6.9 %collective-permute-start.1 = (bf16[520,512]{1,0:T(8,128)(2,1)S(1)}, bf16[520,512]{1,0:T(8,128)(2,1)S(1)}, u32[]{:S(2)}, u32[]{:S(2)}) collective-permute-start(bf16[520,512]{1,0:T(8,128)(2,1)S(1)} %collective-permute-done.a_0_.a_1_), channel_id=1, source_target_pairs={{0,1},{1,0},{2,3},{3,2},{4,5},{5,4},{6,7},{7,6},{8,9},{9,8},{10,11... | collective-permute-start | bytes 1597448 | tf_op jit(solution)/shard_map/ppermute | solution.py:37
  34.3 6.3 %collective-permute-start.3 = (bf16[72,512]{1,0:T(8,128)(2,1)S(1)}, bf16[72,512]{1,0:T(8,128)(2,1)S(1)}, u32[]{:S(2)}, u32[]{:S(2)}) collective-permute-start(bf16[72,512]{1,0:T(8,128)(2,1)S(1)} %own.1.refs_0_.a_1_.a_6_), channel_id=1, source_target_pairs={{352,0},{161,1},{384,32},{193,33},{416,64},{225,65},{448,96},{257,... | collective-permute-start | bytes 221192 | tf_op jit(solution)/shard_map/ppermute | solution.py:37
  40.6 4.4 %collective-permute-done.3.refs_1_.refs_3_.a_3_.refs_2_.a_8_ = bf16[72,512]{1,0:T(8,128)(2,1)S(1)} collective-permute-done((bf16[72,512]{1,0:T(8,128)(2,1)S(1)}, bf16[72,512]{1,0:T(8,128)(2,1)S(1)}, u32[]{:S(2)}, u32[]{:S(2)}) %collective-permute-start.3) | collective-permute-done | bytes 73760 | tf_op jit(solution)/shard_map/ppermute | solution.py:37
  45.1 3.0 %collective-permute-start.6 = (bf16[328,512]{1,0:T(8,128)(2,1)S(1)}, bf16[328,512]{1,0:T(8,128)(2,1)S(1)}, u32[]{:S(2)}, u32[]{:S(2)}) collective-permute-start(bf16[328,512]{1,0:T(8,128)(2,1)S(1)} %shard_map.78), channel_id=1, source_target_pairs={{32,0},{481,1},{64,32},{1,33},{96,64},{33,65},{128,96},{65,97},{16... | collective-permute-start | bytes 1007624 | tf_op jit(solution)/shard_map/ppermute | solution.py:37
  48.2 5.5 %collective-permute-start.5 = (bf16[136,512]{1,0:T(8,128)(2,1)S(1)}, bf16[136,512]{1,0:T(8,128)(2,1)S(1)}, u32[]{:S(2)}, u32[]{:S(2)}) collective-permute-start(bf16[136,512]{1,0:T(8,128)(2,1)S(1)} %shard_map.77), channel_id=1, source_target_pairs={{448,0},{65,1},{480,32},{97,33},{0,64},{129,65},{32,96},{161,97},{... | collective-permute-start | bytes 417800 | tf_op jit(solution)/shard_map/ppermute | solution.py:37
  53.7 3.9 %collective-permute-done.5.a_5_.refs_1_.a_10_ = bf16[136,512]{1,0:T(8,128)(2,1)S(1)} collective-permute-done((bf16[136,512]{1,0:T(8,128)(2,1)S(1)}, bf16[136,512]{1,0:T(8,128)(2,1)S(1)}, u32[]{:S(2)}, u32[]{:S(2)}) %collective-permute-start.5) | collective-permute-done | bytes 139296 | tf_op jit(solution)/shard_map/ppermute | solution.py:37
  57.7 5.7 %collective-permute-start.7 = (bf16[264,512]{1,0:T(8,128)(2,1)S(1)}, bf16[264,512]{1,0:T(8,128)(2,1)S(1)}, u32[]{:S(2)}, u32[]{:S(2)}) collective-permute-start(bf16[264,512]{1,0:T(8,128)(2,1)S(1)} %shard_map.81), channel_id=1, source_target_pairs={{480,0},{33,1},{0,32},{65,33},{32,64},{97,65},{64,96},{129,97},{96... | collective-permute-start | bytes 811016 | tf_op jit(solution)/shard_map/ppermute | solution.py:37
  63.4 1.6 %shard_map.79 = (f32[768,1024]{1,0:T(8,128)S(1)}, f32[1,1024]{1,0:T(1,128)S(1)}, bf16[512,768]{1,0:T(8,128)(2,1)S(1)}, bf16[768,512]{1,0:T(8,128)(2,1)S(1)}, f32[768,128]{1,0:T(8,128)S(1)}) custom-call(bf16[1024,512]{1,0:T(8,128)(2,1)S(1)} %copy-done, bf16[72,512]{1,0:T(8,128)(2,1)S(1)} %own.1.refs_0_.a_1_.a_6_, ...), custom_call_target="tpu_custom_call" | custom-call | flops 805306368 | bytes 4194304 | tf_op jit(solution)/shard_map/pallas_call | solution.py:250
  65.0 1.5 %shard_map.80 = (f32[768,1024]{1,0:T(8,128)S(1)}, f32[1,1024]{1,0:T(1,128)S(1)}, f32[2,8,128]{2,1,0:T(8,128)S(1)}) custom-call(bf16[520,512]{1,0:T(8,128)(2,1)S(1)} %collective-permute-done.a_0_.a_1_, bf16[520,512]{1,0:T(8,128)(2,1)S(1)} %collective-permute-done.1.a_1_.a_2_, f32[1,1024]{1,0:T(1,128)S(1)} %bitcast.7, ...), custom_call_target="tpu_custom_call" | custom-call | flops 805306368 | bytes 4194304 | tf_op jit(solution)/shard_map/pallas_call | solution.py:250
  66.7 1.3 shard_map.82
  68.1 17.0 %all_to_all.15.parts = f32[32,2,8,128]{3,2,1,0:T(8,128)S(1)} all-to-all(f32[32,2,8,128]{3,2,1,0:T(8,128)S(1)} %get-tuple-element.30), channel_id=1, replica_groups=mesh['z'=16,'yh'=2,'yl'=2,'x'=4,'c'=2] {'c','x','yh','yl'}, dimensions={0} | all-to-all | bytes 524288 | tf_op jit(solution)/shard_map/all_to_all | solution.py:498
  85.0 2.1 %cols.1 = (f32[1,2048]{1,0:T(1,128)S(1)}, f32[16,8,128]{2,1,0:T(8,128)S(1)}) custom-call(f32[32,2,8,128]{3,2,1,0:T(8,128)S(1)} %all_to_all.15.parts, f32[2,8,128]{2,1,0:T(8,128)S(1)} %get-tuple-element.31.logs, f32[768,1024]{1,0:T(8,128)S(1)} %get-tuple-element.32.s1, f32[768,1024]{1,0:T(8,128)S(1)} %get-tuple-element.33.s2, ...), custom_call_target="tpu_custom_call" | custom-call | tf_op jit(solution)/shard_map/cols/pallas_call | solution.py:332
  87.2 17.2 %all_to_all.16.parts = f32[16,8,128]{2,1,0:T(8,128)S(1)} all-to-all(f32[16,8,128]{2,1,0:T(8,128)S(1)} %get-tuple-element.35), channel_id=1, replica_groups=mesh['z'=16,'yh'=2,'yl'=2,'x'=4,'c'=2] {'z'}, dimensions={0} | all-to-all | bytes 131072 | tf_op jit(solution)/shard_map/all_to_all | solution.py:500
  104.4 2.3 %moved.1 = (f32[1,128]{1,0:T(1,128)S(1)}, bf16[264,2048]{1,0:T(8,128)(2,1)S(1)}, f32[1,2048]{1,0:T(1,128)S(1)}, bf16[1024,2048]{1,0:T(8,128)(2,1)S(1)}) custom-call(f32[16,8,128]{2,1,0:T(8,128)S(1)} %all_to_all.16.parts, f32[16,128]{1,0:T(8,128)S(1)} %get-tuple-element.36.lt, f32[1,2048]{1,0:T(1,128)S(1)} %get-tuple-element.37.sp, ...), custom_call_target="tpu_custom_call" | custom-call | tf_op jit(solution)/shard_map/moved/pallas_call | solution.py:382
  106.7 3.9 %collective-permute-start.8 = (bf16[264,2048]{1,0:T(8,128)(2,1)S(1)}, bf16[264,2048]{1,0:T(8,128)(2,1)S(1)}, u32[]{:S(2)}, u32[]{:S(2)}) collective-permute-start(bf16[264,2048]{1,0:T(8,128)(2,1)S(1)} %get-tuple-element.39), channel_id=1, source_target_pairs={{0,1},{1,0},{2,3},{3,2},{4,5},{5,4},{6,7},{7,6},{8,9},{9,8},{10,11... | collective-permute-start | bytes 3244040 | tf_op jit(solution)/shard_map/ppermute | solution.py:502
  110.6 1.3 mine.1
  111.9 1.0 collective-permute-done.8.theirs
  113.2 20.2 %all_to_all.17.parts = bf16[16,272,128]{2,1,0:T(8,128)(2,1)S(1)} all-to-all(bf16[16,272,128]{2,1,0:T(8,128)(2,1)S(1)} %pack.1), channel_id=1, replica_groups=mesh['z'=16,'yh'=2,'yl'=2,'x'=4,'c'=2] {'yl','yh','x'}, dimensions={0} | all-to-all | bytes 2228224 | tf_op jit(solution)/shard_map/all_to_all | solution.py:504
  (15 shorter events, 1.7 us)
Async XLA Ops:
  0.6 62.7 %copy-start = (bf16[1024,512]{1,0:T(8,128)(2,1)S(1)}, bf16[1024,512]{1,0:T(8,128)(2,1)}, u32[]{:S(2)}) copy-start(bf16[1024,512]{1,0:T(8,128)(2,1)} %a_0_.3) | copy-start | bytes 3145732
  1.8 25.5 %collective-permute-start = (bf16[520,512]{1,0:T(8,128)(2,1)S(1)}, bf16[520,512]{1,0:T(8,128)(2,1)S(1)}, u32[]{:S(2)}, u32[]{:S(2)}) collective-permute-start(bf16[520,512]{1,0:T(8,128)(2,1)S(1)} %near_message.1), channel_id=1, source_target_pairs={{0,24},{24,0},{8,16},{16,8},{1,25},{25,1},{9,17},{17,9},{2,26},{26... | collective-permute-start | bytes 1597448 | tf_op jit(solution)/shard_map/ppermute | solution.py:37
  8.2 14.5 %collective-permute-start.2 = (bf16[72,512]{1,0:T(8,128)(2,1)S(1)}, bf16[72,512]{1,0:T(8,128)(2,1)S(1)}, u32[]{:S(2)}, u32[]{:S(2)}) collective-permute-start(bf16[72,512]{1,0:T(8,128)(2,1)S(1)} %own.1.refs_0_.a_1_.a_6_), channel_id=1, source_target_pairs={{128,0},{385,1},{160,32},{417,33},{192,64},{449,65},{224,96},{481,... | collective-permute-start | bytes 221192 | tf_op jit(solution)/shard_map/ppermute | solution.py:37
  22.8 42.2 %copy-start.1 = (f32[1024]{0:T(1024)S(1)}, f32[1024]{0:T(1024)}, u32[]{:S(2)}) copy-start(f32[1024]{0:T(1024)} %param.6) | copy-start | bytes 12292
  22.8 22.2 %collective-permute-start.4 = (bf16[136,512]{1,0:T(8,128)(2,1)S(1)}, bf16[136,512]{1,0:T(8,128)(2,1)S(1)}, u32[]{:S(2)}, u32[]{:S(2)}) collective-permute-start(bf16[136,512]{1,0:T(8,128)(2,1)S(1)} %shard_map.76), channel_id=1, source_target_pairs={{64,0},{449,1},{96,32},{481,33},{128,64},{1,65},{160,96},{33,97},{... | collective-permute-start | bytes 417800 | tf_op jit(solution)/shard_map/ppermute | solution.py:37
  27.4 37.6 %collective-permute-start.1 = (bf16[520,512]{1,0:T(8,128)(2,1)S(1)}, bf16[520,512]{1,0:T(8,128)(2,1)S(1)}, u32[]{:S(2)}, u32[]{:S(2)}) collective-permute-start(bf16[520,512]{1,0:T(8,128)(2,1)S(1)} %collective-permute-done.a_0_.a_1_), channel_id=1, source_target_pairs={{0,1},{1,0},{2,3},{3,2},{4,5},{5,4},{6,7},{7,6},{8,9},{9,8},{10,11... | collective-permute-start | bytes 1597448 | tf_op jit(solution)/shard_map/ppermute | solution.py:37
  34.3 10.7 %collective-permute-start.3 = (bf16[72,512]{1,0:T(8,128)(2,1)S(1)}, bf16[72,512]{1,0:T(8,128)(2,1)S(1)}, u32[]{:S(2)}, u32[]{:S(2)}) collective-permute-start(bf16[72,512]{1,0:T(8,128)(2,1)S(1)} %own.1.refs_0_.a_1_.a_6_), channel_id=1, source_target_pairs={{352,0},{161,1},{384,32},{193,33},{416,64},{225,65},{448,96},{257,... | collective-permute-start | bytes 221192 | tf_op jit(solution)/shard_map/ppermute | solution.py:37
  45.1 18.3 %collective-permute-start.6 = (bf16[328,512]{1,0:T(8,128)(2,1)S(1)}, bf16[328,512]{1,0:T(8,128)(2,1)S(1)}, u32[]{:S(2)}, u32[]{:S(2)}) collective-permute-start(bf16[328,512]{1,0:T(8,128)(2,1)S(1)} %shard_map.78), channel_id=1, source_target_pairs={{32,0},{481,1},{64,32},{1,33},{96,64},{33,65},{128,96},{65,97},{16... | collective-permute-start | bytes 1007624 | tf_op jit(solution)/shard_map/ppermute | solution.py:37
  48.2 9.4 %collective-permute-start.5 = (bf16[136,512]{1,0:T(8,128)(2,1)S(1)}, bf16[136,512]{1,0:T(8,128)(2,1)S(1)}, u32[]{:S(2)}, u32[]{:S(2)}) collective-permute-start(bf16[136,512]{1,0:T(8,128)(2,1)S(1)} %shard_map.77), channel_id=1, source_target_pairs={{448,0},{65,1},{480,32},{97,33},{0,64},{129,65},{32,96},{161,97},{... | collective-permute-start | bytes 417800 | tf_op jit(solution)/shard_map/ppermute | solution.py:37
  57.7 9.1 %collective-permute-start.7 = (bf16[264,512]{1,0:T(8,128)(2,1)S(1)}, bf16[264,512]{1,0:T(8,128)(2,1)S(1)}, u32[]{:S(2)}, u32[]{:S(2)}) collective-permute-start(bf16[264,512]{1,0:T(8,128)(2,1)S(1)} %shard_map.81), channel_id=1, source_target_pairs={{480,0},{33,1},{0,32},{65,33},{32,64},{97,65},{64,96},{129,97},{96... | collective-permute-start | bytes 811016 | tf_op jit(solution)/shard_map/ppermute | solution.py:37
  106.7 6.3 %collective-permute-start.8 = (bf16[264,2048]{1,0:T(8,128)(2,1)S(1)}, bf16[264,2048]{1,0:T(8,128)(2,1)S(1)}, u32[]{:S(2)}, u32[]{:S(2)}) collective-permute-start(bf16[264,2048]{1,0:T(8,128)(2,1)S(1)} %get-tuple-element.39), channel_id=1, source_target_pairs={{0,1},{1,0},{2,3},{3,2},{4,5},{5,4},{6,7},{7,6},{8,9},{9,8},{10,11... | collective-permute-start | bytes 3244040 | tf_op jit(solution)/shard_map/ppermute | solution.py:502
